TPU v7x, 8 devices: a whole 2x2x1 slice. The times are simulated.
8 devices in a mesh: rep: 1 (over z), dp: 8 (over x, y, core).
Axes of the slice: x: 2, y: 2, z: 1, core: 2. Of those that a mesh axis runs over, the one named last changes fastest.
Arguments:
- x: bfloat16 [8, 2048, 896], P(('rep', 'dp'))
- dy: bfloat16 [8, 2048, 896], P(('rep', 'dp'))
- w_gate: bfloat16 [2, 896, 4736], replicated
- w_up: bfloat16 [2, 896, 4736], replicated
- w_down: bfloat16 [2, 4736, 896], replicated
- m_w_gate: float32 [2, 896, 4736], replicated
- m_w_up: float32 [2, 896, 4736], replicated
- m_w_down: float32 [2, 4736, 896], replicated
- v_w_gate: float32 [2, 896, 4736], replicated
- v_w_up: float32 [2, 896, 4736], replicated
- v_w_down: float32 [2, 4736, 896], replicated
Outputs:
- output 1: bfloat16 [2, 896, 4736], P('rep')
- output 2: bfloat16 [2, 896, 4736], P('rep')
- output 3: bfloat16 [2, 4736, 896], P('rep')
- output 4: float32 [2, 896, 4736], P('rep')
- output 5: float32 [2, 896, 4736], P('rep')
- output 6: float32 [2, 4736, 896], P('rep')
- output 7: float32 [2, 896, 4736], P('rep')
- output 8: float32 [2, 896, 4736], P('rep')
- output 9: float32 [2, 4736, 896], P('rep')
All inputs are finite; a program needn't handle non-finite values.
Results may differ from a plain program's by a relative error of at most 0.022.
Values are sent between devices in bfloat16 or wider.
A program may use at most 3 GiB of HBM per device.

v0:
```python
import jax
import jax.numpy as jnp
from jax import lax
from jax.sharding import PartitionSpec as P

NAMES = ("w_gate", "w_up", "w_down")


def matmul(a, w):
    return jnp.dot(a, w, preferred_element_type=jnp.float32).astype(jnp.bfloat16)


def normed(h):
    wide = h.astype(jnp.float32)
    scale = lax.rsqrt(jnp.mean(wide**2, -1, keepdims=True) + 1e-6)
    return (wide * scale).astype(jnp.bfloat16)


def layer(h, w):
    a = normed(h)
    gate = jnp.dot(a, w["w_gate"], preferred_element_type=jnp.float32)
    up = jnp.dot(a, w["w_up"], preferred_element_type=jnp.float32)
    return h + matmul((jax.nn.silu(gate) * up).astype(jnp.bfloat16), w["w_down"])


def adamw(w, m, v, g):
    m = 0.9 * m + 0.1 * g
    v = 0.95 * v + 0.05 * g * g
    step = m * lax.rsqrt(v + 1e-8) + 0.1 * w
    return (w - 0.02 * step).astype(jnp.bfloat16), m, v


def clipped(gradients, sum_of_squares, count):
    factor = jnp.minimum(1.0, 0.5 * lax.rsqrt(sum_of_squares / count + 1e-30))
    return [g * factor for g in gradients]


def solution(mesh):
    def step(x, dy, *arrays):
        weights, m, v = (arrays[i : i + 3] for i in (0, 3, 6))
        layers = weights[0].shape[0]
        h, kept = x[0], []
        for number in range(layers):
            kept.append(h)
            h = layer(h, {name: w[number] for name, w in zip(NAMES, weights, strict=True)})
        by_h, summed = dy[0], [None] * layers
        for number in reversed(range(layers)):
            _, back = jax.vjp(lambda w, h: layer(h, w), {name: w[number] for name, w in zip(NAMES, weights, strict=True)}, kept[number])
            by_w, by_h = back(by_h)
            summed[number] = [lax.psum(by_w[name], "dp") for name in NAMES]
        gradients = [jnp.stack([summed[number][i] for number in range(layers)]).astype(jnp.float32) for i in range(3)]
        gradients = clipped(gradients, sum(jnp.sum(g * g) for g in gradients), sum(g.size for g in gradients))
        new = [adamw(w.astype(jnp.float32), m, v, g) for w, m, v, g in zip(weights, m, v, gradients, strict=True)]
        return tuple(one[which] for which in range(3) for one in new)

    return jax.shard_map(
        step,
        mesh=mesh,
        in_specs=(P(("rep", "dp"), None, None),) * 2 + (P(None, None, None),) * 9,
        out_specs=(P("rep", None, None),) * 9,
        check_vma=False,
    )
```

profile of v0, /device:TPU:0, one launch (start us, length us, event | category | flops | bytes accessed | tf_op | source)
XLA Modules:
  0.0 1290.3 jit_solution(3098413511368785087)
XLA Ops:
  7.2 0.0 all-reduce.3.cloned.1.call-start
  7.2 6.1 copy.20
  13.3 2.8 fusion.74
  16.1 0.0 copy-start.7
  16.1 6.2 copy.21
  22.3 27.9 %convolution_convert_fusion.1 = bf16[2048,4736]{1,0:T(8,128)(2,1)} fusion(bf16[2,4736,896]{2,1,0:T(8,128)(2,1)} %param.15, bf16[1,2048,896]{2,1,0:T(8,128)(2,1)} %param.12), kind=kOutput, calls=%fused_computation.61 | convolution fusion | flops 17390895104 | bytes 31555584 | tf_op jit(solution)/shard_map/transpose(jvp())/dot_general | solution.py:10
  50.2 29.2 %fusion.55 = f32[2048,4736]{1,0:T(8,128)} fusion(bf16[2,896,4736]{2,1,0:T(8,128)(2,1)} %param.13, bf16[1,2048,896]{2,1,0:T(8,128)(2,1)} %param.11, f32[2048]{0:T(1024)S(1)} %add_rsqrt_fusion), kind=kOutput, calls=%fused_computation.91 | convolution fusion | flops 17386700800 | bytes 50962432 | tf_op jit(solution)/shard_map/dot_general | solution.py:21
  79.3 0.0 copy-done.7
  79.3 42.0 %multiply_convert_fusion.1 = (bf16[2048,4736]{1,0:T(8,128)(2,1)}, f32[2048,4736]{1,0:T(8,128)}) fusion(f32[2048,4736]{1,0:T(8,128)} %fusion.55, bf16[2,896,4736]{2,1,0:T(8,128)(2,1)} %param.14, bf16[1,2048,896]{2,1,0:T(8,128)(2,1)} %param.11, f32[2048]{0:T(1024)S(1)} %add_rsqrt_fusion), kind=kOutput, calls=%fused_computation.35 | convolution fusion | flops 17444896768 | bytes 109158400 | tf_op jit(solution)/shard_map/dot_general | solution.py:22
  121.4 24.2 %fusion.78 = (f32[2048]{0:T(1024)S(1)}, bf16[2048,896]{0,1:T(8,128)(2,1)S(1)}) fusion(bf16[2048,4736]{1,0:T(8,128)(2,1)} %get-tuple-element.24, bf16[2,4736,896]{2,1,0:T(8,128)(2,1)} %param.15, bf16[1,2048,896]{1,2,0:T(8,128)(2,1)} %copy.20), kind=kOutput, calls=%fused_computation.112 | convolution fusion | flops 17390368768 | bytes 35233792 | tf_op jit(solution)/shard_map/dot_general | solution.py:10
  145.6 0.0 copy-start.2
  145.6 0.0 copy-start.5
  145.6 29.0 %fusion.42 = f32[2048,4736]{1,0:T(8,128)} fusion(bf16[2,896,4736]{2,1,0:T(8,128)(2,1)} %param.14, bf16[2048,896]{0,1:T(8,128)(2,1)S(1)} %get-tuple-element.27, f32[2048]{0:T(1024)S(1)} %fusion.98), kind=kOutput, calls=%fused_computation.78 | convolution fusion | flops 17386700800 | bytes 50962432 | tf_op jit(solution)/shard_map/jvp()/dot_general | solution.py:22
  174.6 0.0 copy-done.2
  174.6 0.0 copy-done.5
  174.6 50.0 %fusion.5 = (bf16[2048,4736]{1,0:T(8,128)(2,1)}, f32[2048,4736]{1,0:T(8,128)}) fusion(f32[2048,4736]{1,0:T(8,128)} %fusion.42, bf16[2048,4736]{1,0:T(8,128)(2,1)} %convolution_convert_fusion.1, bf16[2,896,4736]{2,1,0:T(8,128)(2,1)} %param.13, bf16[2048,896]{0,1:T(8,128)(2,1)S(1)} %get-tuple-element.27, f32[2048]{0:T(1024)S(1)} %fusion.98), kind=kOutput, calls=%fused_computation.26 | convolution fusion | flops 17503092736 | bytes 128557056 | tf_op jit(solution)/shard_map/jvp()/dot_general | solution.py:21
  224.6 29.8 %fusion.33 = bf16[2048,896]{0,1:T(8,128)(2,1)} fusion(bf16[2048,4736]{1,0:T(8,128)(2,1)} %convolution_convert_fusion.1, bf16[2,896,4736]{2,1,0:T(8,128)(2,1)} %param.14, f32[2048,4736]{1,0:T(8,128)} %get-tuple-element.29), kind=kOutput, calls=%fused_computation.57 | convolution fusion | flops 17439391744 | bytes 70352896 | tf_op jit(solution)/shard_map/transpose(jvp())/dot_general | solution.py:22
  254.4 30.3 %fusion.66 = bf16[1,896,4736]{2,1,0:T(8,128)(2,1)} fusion(bf16[2048,4736]{1,0:T(8,128)(2,1)} %convolution_convert_fusion.1, bf16[2048,896]{0,1:T(8,128)(2,1)} %copy-done.2, f32[2048]{0:T(1024)S(1)} %fusion.98, f32[2048,4736]{1,0:T(8,128)} %get-tuple-element.29), kind=kOutput, calls=%fused_computation.100 | convolution fusion | flops 17449140224 | bytes 70361088 | tf_op jit(solution)/shard_map/transpose(jvp())/dot_general | solution.py:22
  284.7 36.1 %fusion.67 = bf16[1,4736,896]{2,1,0:T(8,128)(2,1)} fusion(f32[2048,4736]{1,0:T(8,128)} %fusion.42, bf16[1,2048,896]{2,1,0:T(8,128)(2,1)} %param.12, f32[2048,4736]{1,0:T(8,128)} %get-tuple-element.29), kind=kOutput, calls=%fused_computation.101 | convolution fusion | flops 17443635200 | bytes 89751552 | tf_op jit(solution)/shard_map/transpose(jvp())/dot_general | solution.py:10
  320.8 0.0 copy-start.3
  320.8 24.6 %fusion.60 = bf16[1,896,4736]{2,1,0:T(8,128)(2,1)} fusion(bf16[2048,4736]{1,0:T(8,128)(2,1)} %get-tuple-element.28, bf16[2048,896]{0,1:T(8,128)(2,1)} %copy-done.2, f32[2048]{0:T(1024)S(1)} %fusion.98), kind=kOutput, calls=%fused_computation.96 | convolution fusion | flops 17386700800 | bytes 31563776 | tf_op jit(solution)/shard_map/transpose(jvp())/dot_general | solution.py:21
  345.4 0.0 copy-done.3
  345.4 0.0 copy-start.6
  345.4 0.0 copy-start.1
  345.4 24.7 %fusion.80 = (f32[2048]{0:T(1024)S(1)}, bf16[2048,896]{0,1:T(8,128)(2,1)S(1)}) fusion(bf16[2048,896]{0,1:T(8,128)(2,1)S(1)} %copy-done.3, bf16[2048,896]{0,1:T(8,128)(2,1)} %fusion.33, bf16[2048,4736]{1,0:T(8,128)(2,1)} %get-tuple-element.28, bf16[2,896,4736]{2,1,0:T(8,128)(2,1)} %param.13), kind=kOutput, calls=%fused_computation.114 | convolution fusion | flops 17390368768 | bytes 38903808 | tf_op jit(solution)/shard_map/transpose(jvp())/dot_general | solution.py:21
  370.1 0.0 copy-done.6
  370.2 0.0 copy-done.1
  370.2 4.9 fusion.83
  375.0 0.0 copy-start.4
  375.0 27.6 %convolution_convert_fusion = bf16[2048,4736]{1,0:T(8,128)(2,1)} fusion(bf16[2048,896]{0,1:T(8,128)(2,1)} %fusion.83, bf16[2,4736,896]{2,1,0:T(8,128)(2,1)} %param.15), kind=kOutput, calls=%fused_computation.60 | convolution fusion | flops 17390895104 | bytes 31555584 | tf_op jit(solution)/shard_map/transpose(jvp())/dot_general | solution.py:10
  402.6 0.0 copy-done.4
  402.6 0.0 copy-start.8
  402.6 26.5 %fusion.61 = bf16[1,4736,896]{2,1,0:T(8,128)(2,1)} fusion(bf16[2048,4736]{1,0:T(8,128)(2,1)} %get-tuple-element.24, bf16[2048,896]{0,1:T(8,128)(2,1)S(1)} %copy-done.4), kind=kOutput, calls=%fused_computation.97 | convolution fusion | flops 17385439232 | bytes 31555584 | tf_op jit(solution)/shard_map/transpose(jvp())/dot_general | solution.py:10
  429.1 0.0 copy-done.8
  429.1 30.4 %fusion.62 = bf16[1,896,4736]{2,1,0:T(8,128)(2,1)} fusion(bf16[2048,4736]{1,0:T(8,128)(2,1)} %convolution_convert_fusion, f32[2048,4736]{1,0:T(8,128)} %fusion.55, bf16[1,2048,896]{1,2,0:T(8,128)(2,1)} %copy.20, f32[2048]{0:T(1024)S(1)} %copy-done.8), kind=kOutput, calls=%fused_computation.98 | convolution fusion | flops 17449140224 | bytes 70361088 | tf_op jit(solution)/shard_map/transpose(jvp())/dot_general | solution.py:22
  459.5 38.3 %fusion.63 = bf16[1,896,4736]{2,1,0:T(8,128)(2,1)} fusion(f32[2048,4736]{1,0:T(8,128)} %fusion.55, f32[2048,4736]{1,0:T(8,128)} %get-tuple-element.25, bf16[2048,4736]{1,0:T(8,128)(2,1)} %convolution_convert_fusion, bf16[1,2048,896]{1,2,0:T(8,128)(2,1)} %copy.20, f32[2048]{0:T(1024)S(1)} %copy-done.8), kind=kOutput, calls=%fused_computation.99 | convolution fusion | flops 17497636864 | bytes 109158400 | tf_op jit(solution)/shard_map/transpose(jvp())/dot_general | solution.py:21
  497.8 0.0 all-reduce.3.cloned.1.call-update
  497.8 575.7 %all-reduce.3.cloned.1.call-done = (bf16[1,896,4736]{2,1,0:T(8,128)(2,1)}, bf16[1,896,4736]{2,1,0:T(8,128)(2,1)}, bf16[1,896,4736]{2,1,0:T(8,128)(2,1)}, bf16[1,...) async-done(((bf16[1,896,4736]{2,1,0:T(8,128)(2,1)}, bf16[1,896,4736]{2,1,0:T(8,128)(2,1)}, bf16[1,896,4736]{2,1,0:T(8,128)(2,1)}, ...) | async-done | bytes 50921488 | tf_op jit(solution)/shard_map/psum | solution.py:50
  1073.5 0.0 slice-start
  1073.5 0.0 copy-start
  1073.5 0.0 slice-start.1
  1073.5 0.0 slice-start.2
  1073.5 11.6 fusion.20
  1085.1 0.0 slice-done
  1085.1 0.0 copy-done
  1085.1 0.0 slice-done.1
  1085.1 0.0 slice-done.2
  1085.1 9.4 fusion.21
  1095.8 11.3 fusion.22
  1107.8 58.2 %fusion.28 = (bf16[2,4736,896]{2,1,0:T(8,128)(2,1)}, f32[2,4736,896]{2,1,0:T(8,128)}, f32[2,4736,896]{2,1,0:T(8,128)}) fusion(bf16[2,4736,896]{2,1,0:T(8,128)(2,1)} %param.15, f32[]{:T(128)S(6)} %min_shard_map.3, bf16[1,4736,896]{2,1,0:T(8,128)(2,1)} %get-tuple-element.13, bf16[1,4736,896]{2,1,0:T(8,128)(2,1)} %get-tuple-element.14, ...), kind=kLoop, calls=%fused_computation.52 | loop fusion | flops 169738240 | bytes 186712064 | tf_op jit(solution)/shard_map/convert_element_type | solution.py:30
  1166.0 117.0 %fusion.19 = (bf16[2,896,4736]{2,1,0:T(8,128)(2,1)}, f32[2,896,4736]{2,1,0:T(8,128)}, f32[2,896,4736]{2,1,0:T(8,128)}, bf16[2,896,4736]{2,1,0:T(8,128)(2,1)}, f3...) fusion(bf16[2,896,4736]{2,1,0:T(8,128)(2,1)} %param.13, f32[]{:T(128)S(6)} %min_shard_map.3, ...), kind=kLoop, calls=%fused_computation.43 | loop fusion | flops 339476480 | bytes 373424128 | tf_op jit(solution)/shard_map/convert_element_type | solution.py:30
  (4 shorter events, 0.0 us)
Async XLA Ops:
  7.2 1066.3 %all-reduce.3.cloned.1.call-start = ((), (), s32[]{:S(2)}) async-start(), calls=%async_computation | async-start | bytes 101842944 | tf_op jit(solution)/shard_map/psum | solution.py:50
  16.1 63.2 %copy-start.7 = (f32[2048]{0:T(1024)}, f32[2048]{0:T(1024)S(1)}, u32[]{:S(2)}) copy-start(f32[2048]{0:T(1024)S(1)} %add_rsqrt_fusion) | copy-start | bytes 24580
  145.6 29.0 %copy-start.2 = (bf16[2048,896]{0,1:T(8,128)(2,1)}, bf16[2048,896]{0,1:T(8,128)(2,1)S(1)}, u32[]{:S(2)}) copy-start(bf16[2048,896]{0,1:T(8,128)(2,1)S(1)} %get-tuple-element.27) | copy-start | bytes 11010052
  145.6 29.0 %copy-start.5 = (f32[2048]{0:T(1024)}, f32[2048]{0:T(1024)S(1)}, u32[]{:S(2)}) copy-start(f32[2048]{0:T(1024)S(1)} %get-tuple-element.26) | copy-start | bytes 24580
  320.8 24.6 %copy-start.3 = (bf16[2048,896]{0,1:T(8,128)(2,1)S(1)}, bf16[2048,896]{0,1:T(8,128)(2,1)}, u32[]{:S(2)}) copy-start(bf16[2048,896]{0,1:T(8,128)(2,1)} %copy-done.2) | copy-start | bytes 11010052
  345.4 24.7 %copy-start.6 = (f32[2048]{0:T(1024)S(1)}, f32[2048]{0:T(1024)}, u32[]{:S(2)}) copy-start(f32[2048]{0:T(1024)} %copy-done.5) | copy-start | bytes 24580
  345.4 24.8 %copy-start.1 = (bf16[1,2048,896]{1,2,0:T(8,128)(2,1)S(1)}, bf16[1,2048,896]{1,2,0:T(8,128)(2,1)}, u32[]{:S(2)}) copy-start(bf16[1,2048,896]{1,2,0:T(8,128)(2,1)} %copy.21) | copy-start | bytes 11010052
  375.0 27.6 %copy-start.4 = (bf16[2048,896]{0,1:T(8,128)(2,1)S(1)}, bf16[2048,896]{0,1:T(8,128)(2,1)}, u32[]{:S(2)}) copy-start(bf16[2048,896]{0,1:T(8,128)(2,1)} %fusion.83) | copy-start | bytes 11010052
  402.6 26.5 %copy-start.8 = (f32[2048]{0:T(1024)S(1)}, f32[2048]{0:T(1024)}, u32[]{:S(2)}) copy-start(f32[2048]{0:T(1024)} %copy-done.7) | copy-start | bytes 24580
  1073.5 11.6 slice-start
  1073.5 11.6 copy-start
  1073.5 11.6 slice-start.1
  1073.5 11.6 slice-start.2
Sparse Core Ops, SparseCore 0:
  497.9 575.5 all-reduce.2
where the time goes:
time: 1300 us; the launch traced here: 1290 us
  waiting for transfers between devices  576 us (44%)
  matrix products  471 us (36%)
  other arithmetic  215 us (17%)
  between operations  16.6 us (1%)
    psum x1, waiting for transfers between devices, step(): summed[number] = [lax.psum(by_w[name], 'dp') for name in NAMES]  576 us
    convert_element_type x2, other arithmetic, adamw(): return ((w - 0.02 * step).astype(jnp.bfloat16), m, v)  175 us
    dot_general x5, matrix products, layer(): gate = jnp.dot(a, w['w_gate'], preferred_element_type=jnp.float32)  167 us
    dot_general x5, matrix products, layer(): up = jnp.dot(a, w['w_up'], preferred_element_type=jnp.float32)  161 us
    dot_general x5, matrix products, matmul(): jnp.dot(a, w, preferred_element_type=jnp.float32).astype(jnp.bfloat16)  142 us
    reduce_sum x3, other arithmetic, step(): jnp.sum(g * g)  32.3 us
  transfers between devices with their start and end apart: 1, of which 1 were waited for; matrix products, arithmetic and copies ran while one was open for 0% of the time, Pallas kernels for 0%

commit v1 on v0

v1 whole, which is shorter than its diff:
```python
import functools

import jax
import jax.numpy as jnp
from jax import lax
from jax.experimental import pallas as pl
from jax.experimental.pallas import tpu as pltpu
from jax.sharding import PartitionSpec as P

BF, F32 = jnp.bfloat16, jnp.float32
FC = 256
TM = 512
LIMIT = 62 * 1024 * 1024
SPREAD = 10
LAG = 2
SLOTS = 4


def normed(h):
    wide = h.astype(F32)
    scale = lax.rsqrt(jnp.mean(wide**2, -1, keepdims=True) + 1e-6)
    return (wide * scale).astype(BF)


def nt(a, b):
    return lax.dot_general(a, b, (((1,), (1,)), ((), ())), preferred_element_type=F32)


def nn(a, b):
    return jnp.dot(a, b, preferred_element_type=F32)


def masked(c, width, axis, w):
    place = lax.broadcasted_iota(jnp.int32, w.shape, axis) + c * FC
    return jnp.where(place < width, w, jnp.zeros_like(w))


def once(shape):
    return pl.BlockSpec(shape, lambda c: (0,) * len(shape), pipeline_mode=pl.Buffered(1))


def params(**more):
    return pltpu.CompilerParams(vmem_limit_bytes=LIMIT, dimension_semantics=("arbitrary",), **more)


def fwd_body(width, x_ref, wg_ref, wu_ref, wd_ref, g_ref, u_ref, h_ref, a_ref, acc, ws, wds):
    c = pl.program_id(0)

    @pl.when(c == 0)
    def _():
        acc[...] = jnp.zeros_like(acc)
        a_ref[...] = normed(x_ref[...])

    ws[:, :FC] = masked(c, width, 1, wg_ref[...])
    ws[:, FC:] = masked(c, width, 1, wu_ref[...])
    wds[...] = masked(c, width, 0, wd_ref[...])

    def tile(i, _):
        rows = pl.ds(pl.multiple_of(i * TM, TM), TM)
        gu = nn(a_ref[rows, :], ws[...])
        g, u = gu[:, :FC], gu[:, FC:]
        g_ref[rows, :] = g
        u_ref[rows, :] = u
        acc[rows, :] += nn((g * jax.nn.sigmoid(g) * u).astype(BF), wds[...])
        return 0

    lax.fori_loop(0, a_ref.shape[0] // TM, tile, 0, unroll=True)

    @pl.when(c == pl.num_programs(0) - 1)
    def _():
        h_ref[...] = x_ref[...] + acc[...].astype(BF)


def forward(layer, x, w_gate, w_up, w_down):
    t, d = x.shape
    f = w_gate.shape[2]
    n = pl.cdiv(f, FC)
    wcol = pl.BlockSpec((None, d, FC), lambda c: (layer, 0, c))
    wrow = pl.BlockSpec((None, FC, d), lambda c: (layer, c, 0))
    return pl.pallas_call(
        functools.partial(fwd_body, f),
        grid=(n,),
        in_specs=[once((t, d)), wcol, wcol, wrow],
        out_specs=[pl.BlockSpec((t, FC), lambda c: (0, c))] * 2 + [once((t, d))],
        out_shape=[jax.ShapeDtypeStruct((t, n * FC), F32)] * 2 + [jax.ShapeDtypeStruct((t, d), BF)],
        scratch_shapes=[pltpu.VMEM((t, d), BF), pltpu.VMEM((t, d), F32), pltpu.VMEM((d, 2 * FC), BF), pltpu.VMEM((FC, d), BF)],
        compiler_params=params(),
        cost_estimate=pl.CostEstimate(flops=6 * t * d * f, bytes_accessed=10 * t * f, transcendentals=t * f),
        name="forward",
    )(x, w_gate, w_up, w_down)


class Sum:
    def __init__(self, n, rows, out_ref, ss_ref, refs, spread=0, whole_ref=None):
        self.n, self.rows, self.out, self.ss = n, rows, out_ref, ss_ref
        self.spread, self.whole = spread, whole_ref
        self.own, self.land0, self.send1, self.keep1, self.land1, self.send2, self.keep2, self.land2 = refs[:8]
        self.sends, self.lands = refs[8:14:2], refs[9:14:2]
        if spread:
            self.fin, self.local, *sems = refs[14:]
            self.out_sends, self.out_lands = sems[::2], sems[1::2]
        me = self.me = lax.axis_index("dp")
        self.x, self.y, self.core = me // 4, (me // 2) % 2, me % 2
        self.over = (me + 1 - 2 * self.core, me + 4 - 8 * self.x, me + 2 - 4 * self.y)

    @staticmethod
    def scratch(rows):
        def buffer(slots, *shape, dtype=BF):
            return pltpu.VMEM((slots, *shape, rows, FC), dtype)

        return [
            buffer(2, 2, 3, 4),
            buffer(SLOTS, 3, 4),
            buffer(2, 3, 2),
            buffer(2, 3, 2, dtype=F32),
            buffer(SLOTS, 3, 2),
            buffer(2, 3),
            buffer(2, 3, dtype=F32),
            buffer(SLOTS, 3),
        ] + [pltpu.SemaphoreType.DMA((2,)), pltpu.SemaphoreType.DMA((SLOTS,))] * 3

    @staticmethod
    def spread_scratch(rows):
        sems = [pltpu.SemaphoreType.DMA((slots, copies)) for copies in (1, 2, 4) for slots in (2, SLOTS)]
        return [pltpu.VMEM((2, 3, rows, FC), BF), pltpu.SemaphoreType.DMA((2,)), *sems]

    def enter(self):
        barrier = pltpu.get_barrier_semaphore()
        for other in self.over:
            pl.semaphore_signal(barrier, inc=1, device_id={"dp": other}, device_id_type=pl.DeviceIdType.MESH)
        pl.semaphore_wait(barrier, 3)

    def put(self, c, which, g):
        slot = lax.rem(c, 2)
        for j in range(8):
            core, x, y = (j % 2 + self.core) % 2, (j // 4 + self.x) % 2, ((j // 2) % 2 + self.y) % 2
            self.own[slot, core, which, x * 2 + y] = g[j * self.rows : (j + 1) * self.rows].astype(BF)

    def copy(self, stage, k):
        two, four, odd = lax.rem(k, 2), lax.rem(k, SLOTS), lax.rem(k, 2)
        if stage == 0:
            src, dst, to = self.own.at[two, 1], self.land0.at[four], self.over[0]
        elif stage == 1:
            src, dst, to = self.send1.at[two], self.land1.at[four], self.over[1] * (1 - odd) + self.over[2] * odd
        else:
            src, dst, to = self.send2.at[two], self.land2.at[four], self.over[2] * (1 - odd) + self.over[1] * odd
        return pltpu.make_async_remote_copy(
            src_ref=src,
            dst_ref=dst,
            send_sem=self.sends[stage].at[two],
            recv_sem=self.lands[stage].at[four],
            device_id={"dp": to},
            device_id_type=pl.DeviceIdType.MESH,
        )

    def when(self, k, n=None):
        return pl.when((k >= 0) & (k < (self.n if n is None else n)))

    def keep(self, k):
        return pltpu.make_async_copy(self.fin.at[lax.rem(k, 2)], self.whole.at[self.me, k], self.local.at[lax.rem(k, 2)])

    def give(self, stage, k):
        two, four, odd = lax.rem(k, 2), lax.rem(k, SLOTS), lax.rem(k, 2)
        near = self.over[1] * (1 - odd) + self.over[2] * odd
        far = self.over[2] * (1 - odd) + self.over[1] * odd
        blocks = (self.me, far, near, near + far - self.me)[: 2**stage]
        to = (far, near, self.over[0])[stage]
        return [
            pltpu.make_async_remote_copy(
                src_ref=self.whole.at[block, k] if stage else self.fin.at[two],
                dst_ref=self.whole.at[block, k],
                send_sem=self.out_sends[stage].at[two, i],
                recv_sem=self.out_lands[stage].at[four, i],
                device_id={"dp": to},
                device_id_type=pl.DeviceIdType.MESH,
            )
            for i, block in enumerate(blocks)
        ]

    def receive(self, c):
        for stage in (2, 1, 0) if self.spread else ():
            k = c - (4 + stage) * LAG

            @self.when(k, self.spread)
            def _(stage=stage, k=k):
                if stage == 0:
                    self.keep(k).wait()
                for copy in self.give(stage, k):
                    copy.wait()

        k2 = c - 3 * LAG

        @self.when(k2)
        def _():
            self.copy(2, k2).wait()
            g = (self.keep2[lax.rem(k2, 2)] + self.land2[lax.rem(k2, SLOTS)].astype(F32)).astype(BF)
            self.out[...] = g
            if self.spread:
                self.fin[lax.rem(k2, 2)] = g
            g = g.astype(F32)
            self.ss[...] += g[0] * g[0] + g[1] * g[1] + g[2] * g[2]

        k1 = c - 2 * LAG

        @self.when(k1)
        def _():
            self.copy(1, k1).wait()
            two, four = lax.rem(k1, 2), lax.rem(k1, SLOTS)
            self.keep2[two] = self.keep1[two, :, 0] + self.land1[four, :, 0].astype(F32)
            self.send2[two] = (self.keep1[two, :, 1] + self.land1[four, :, 1].astype(F32)).astype(BF)

        k0 = c - LAG

        @self.when(k0)
        def _():
            self.copy(0, k0).wait()
            two, four = lax.rem(k0, 2), lax.rem(k0, SLOTS)
            odd = two
            for to, place in ((0, 0), (1, 1 + odd)):
                self.keep1[two, :, to] = self.own[two, 0, :, place].astype(F32) + self.land0[four, :, place].astype(F32)
            for to, place in ((0, 2 - odd), (1, 3)):
                self.send1[two, :, to] = (self.own[two, 0, :, place].astype(F32) + self.land0[four, :, place].astype(F32)).astype(BF)

    def send(self, c):
        for stage in range(3):
            k = c - stage * LAG

            @self.when(k)
            def _(stage=stage, k=k):
                self.copy(stage, k).start()

        for stage in range(3 if self.spread else 0):
            k = c - (3 + stage) * LAG

            @self.when(k, self.spread)
            def _(stage=stage, k=k):
                if stage == 0:
                    self.keep(k).start()
                for copy in self.give(stage, k):
                    copy.start()


def back(g, u, dh):
    s = jax.nn.sigmoid(g)
    silu = g * s
    return (silu * u).astype(BF), (dh * u * (s + silu * (1 - s))).astype(BF), (dh * silu).astype(BF)


def gradients(total, c, at_ref, dyt_ref, dgu, hid):
    o = nn(at_ref[...], dgu[...])
    total.put(c, 0, o[:, :FC])
    total.put(c, 1, o[:, FC:])
    total.put(c, 2, nn(dyt_ref[...], hid[...]))


def turn(to_ref, of):
    for i in range(to_ref.shape[1] // TM):
        rows = pl.ds(i * TM, TM)
        to_ref[:, rows] = of(rows).T


def by_normed(h, by_a):
    h, by_a = h.astype(F32), by_a.astype(BF).astype(F32)
    scale = lax.rsqrt(jnp.mean(h**2, -1, keepdims=True) + 1e-6)
    return (by_a * scale - h * (scale**3 * jnp.mean(by_a * h, -1, keepdims=True))).astype(BF)


def last_body(width, n, h_ref, dy_ref, wg_ref, wu_ref, wd_ref, out_ref, ss_ref, by_ref, whole_ref, a_ref, at_ref, dyt_ref, da_ref, ws, wds, dgu, hid, *refs):
    c = pl.program_id(0)
    total = Sum(n, out_ref.shape[1], out_ref, ss_ref, refs, SPREAD, whole_ref)

    @pl.when(c == 0)
    def _():
        total.enter()
        da_ref[...] = jnp.zeros_like(da_ref)
        ss_ref[...] = jnp.zeros_like(ss_ref)
        a_ref[...] = normed(h_ref[...])
        turn(at_ref, lambda rows: a_ref[rows, :])
        turn(dyt_ref, lambda rows: dy_ref[rows, :])

    total.receive(c)

    @pl.when(c < n)
    def _():
        ws[:, :FC] = masked(c, width, 1, wg_ref[...])
        ws[:, FC:] = masked(c, width, 1, wu_ref[...])
        wds[...] = masked(c, width, 0, wd_ref[...])

        def tile(i, _):
            rows = pl.ds(pl.multiple_of(i * TM, TM), TM)
            gu = nn(a_ref[rows, :], ws[...])
            dh = nt(dy_ref[rows, :], wds[...]).astype(BF).astype(F32)
            h, dg, du = back(gu[:, :FC], gu[:, FC:], dh)
            hid[rows, :] = h
            dgu[rows, :FC] = dg
            dgu[rows, FC:] = du
            da_ref[rows, :] += nt(dgu[rows, :], ws[...])
            return 0

        lax.fori_loop(0, a_ref.shape[0] // TM, tile, 0, unroll=True)
        gradients(total, c, at_ref, dyt_ref, dgu, hid)

    total.send(c)

    @pl.when(c == n)
    def _():
        def tile(i, _):
            rows = pl.ds(pl.multiple_of(i * TM, TM), TM)
            by_ref[rows, :] = dy_ref[rows, :] + by_normed(h_ref[rows, :], da_ref[rows, :])
            return 0

        lax.fori_loop(0, by_ref.shape[0] // TM, tile, 0)


def last(layer, h, dy, w_gate, w_up, w_down):
    t, d = h.shape
    f = w_gate.shape[2]
    n = pl.cdiv(f, FC)
    rows = d // 8
    wcol = pl.BlockSpec((None, d, FC), lambda c: (layer, 0, jnp.minimum(c, n - 1)))
    wrow = pl.BlockSpec((None, FC, d), lambda c: (layer, jnp.minimum(c, n - 1), 0))
    return pl.pallas_call(
        functools.partial(last_body, f, n),
        grid=(n + 3 * LAG,),
        in_specs=[once((t, d)), once((t, d)), wcol, wcol, wrow],
        out_specs=[
            pl.BlockSpec((None, 3, rows, FC), lambda c: (jnp.maximum(c - 3 * LAG, 0), 0, 0, 0)),
            pl.BlockSpec((rows, FC), lambda c: (0, 0)),
            once((t, d)),
            pl.BlockSpec(memory_space=pl.ANY),
        ],
        out_shape=[
            jax.ShapeDtypeStruct((n, 3, rows, FC), BF),
            jax.ShapeDtypeStruct((rows, FC), F32),
            jax.ShapeDtypeStruct((t, d), BF),
            jax.ShapeDtypeStruct((8, SPREAD, 3, rows, FC), BF),
        ],
        scratch_shapes=[
            pltpu.VMEM((t, d), BF),
            pltpu.VMEM((d, t), BF),
            pltpu.VMEM((d, t), BF),
            pltpu.VMEM((t, d), F32),
            pltpu.VMEM((d, 2 * FC), BF),
            pltpu.VMEM((FC, d), BF),
            pltpu.VMEM((t, 2 * FC), BF),
            pltpu.VMEM((t, FC), BF),
            *Sum.scratch(rows),
            *Sum.spread_scratch(rows),
        ],
        compiler_params=params(collective_id=0, has_side_effects=True),
        cost_estimate=pl.CostEstimate(flops=16 * t * d * f, bytes_accessed=10 * d * f, transcendentals=t * f),
        name="last",
    )(h, dy, w_gate, w_up, w_down)


def first_body(width, n, x_ref, dy_ref, g_ref, u_ref, wd_ref, so_far_ref, out_ref, sum_ref, ss_ref, at_ref, dyt_ref, wds, dgu, hid, part, landed, part_sent, part_landed, *refs):
    c = pl.program_id(0)
    total = Sum(n, out_ref.shape[1], out_ref, ss_ref, refs)

    @pl.when(c == 0)
    def _():
        total.enter()
        ss_ref[...] = so_far_ref[...]
        turn(at_ref, lambda rows: normed(x_ref[rows, :]))
        turn(dyt_ref, lambda rows: dy_ref[rows, :])

    total.receive(c)

    @pl.when(c < n)
    def _():
        wds[...] = masked(c, width, 0, wd_ref[...])

        def tile(i, _):
            rows = pl.ds(pl.multiple_of(i * TM, TM), TM)
            dh = nt(dy_ref[rows, :], wds[...]).astype(BF).astype(F32)
            h, dg, du = back(g_ref[rows, :], u_ref[rows, :], dh)
            hid[rows, :] = h
            dgu[rows, :FC] = dg
            dgu[rows, FC:] = du
            return 0

        lax.fori_loop(0, dy_ref.shape[0] // TM, tile, 0, unroll=True)
        gradients(total, c, at_ref, dyt_ref, dgu, hid)

    total.send(c)

    @pl.when(c == n + 3 * LAG - 1)
    def _():
        part[0] = jnp.full(part.shape[1:], jnp.sum(ss_ref[...]))
        for stage in range(3):
            copy = pltpu.make_async_remote_copy(
                src_ref=part.at[stage],
                dst_ref=landed.at[stage],
                send_sem=part_sent.at[stage],
                recv_sem=part_landed.at[stage],
                device_id={"dp": total.over[stage]},
                device_id_type=pl.DeviceIdType.MESH,
            )
            copy.start()
            copy.wait()
            part[stage + 1] = part[stage] + landed[stage]
        sum_ref[...] = part[3]


def first(layer, x, dy, g, u, w_down, so_far):
    t, d = dy.shape
    f = w_down.shape[1]
    n = pl.cdiv(f, FC)
    rows = d // 8
    gu = pl.BlockSpec((t, FC), lambda c: (0, jnp.minimum(c, n - 1)))
    wrow = pl.BlockSpec((None, FC, d), lambda c: (layer, jnp.minimum(c, n - 1), 0))
    return pl.pallas_call(
        functools.partial(first_body, f, n),
        grid=(n + 3 * LAG,),
        in_specs=[once((t, d)), once((t, d)), gu, gu, wrow, once((rows, FC))],
        out_specs=[
            pl.BlockSpec((None, 3, rows, FC), lambda c: (jnp.maximum(c - 3 * LAG, 0), 0, 0, 0)),
            once((8, 128)),
        ],
        out_shape=[jax.ShapeDtypeStruct((n, 3, rows, FC), BF), jax.ShapeDtypeStruct((8, 128), F32)],
        scratch_shapes=[
            pltpu.VMEM((rows, FC), F32),
            pltpu.VMEM((d, t), BF),
            pltpu.VMEM((d, t), BF),
            pltpu.VMEM((FC, d), BF),
            pltpu.VMEM((t, 2 * FC), BF),
            pltpu.VMEM((t, FC), BF),
            pltpu.VMEM((4, 8, 128), F32),
            pltpu.VMEM((3, 8, 128), F32),
            pltpu.SemaphoreType.DMA((3,)),
            pltpu.SemaphoreType.DMA((3,)),
            *Sum.scratch(rows),
        ],
        compiler_params=params(collective_id=1, has_side_effects=True),
        cost_estimate=pl.CostEstimate(flops=8 * t * d * f, bytes_accessed=8 * t * f, transcendentals=t * f),
        name="first",
    )(x, dy, g, u, w_down, so_far)


def adamw_body(count, sum_ref, g_ref, *refs):
    ins, outs = refs[:9], refs[-9:]
    factor = jnp.minimum(1.0, 0.5 * lax.rsqrt(sum_ref[0:1, 0:1] / count + 1e-30))
    for i in range(3):
        w_ref, m_ref, v_ref = ins[i::3]
        w_out, m_out, v_out = outs[i::3]
        g = g_ref[:, i].reshape(-1, FC)
        g = (g.T if i == 2 else g).astype(F32) * factor
        m = 0.9 * m_ref[...] + 0.1 * g
        v = 0.95 * v_ref[...] + 0.05 * g * g
        w = w_ref[...].astype(F32)
        m_out[...] = m
        v_out[...] = v
        w_out[...] = (w - 0.02 * (m * lax.rsqrt(v + 1e-8) + 0.1 * w)).astype(BF)


def adamw(layer, start, squares, g, w, m, v, done):
    d, f = w[0].shape[1:]
    chunks = g.shape[1]
    wide = pl.BlockSpec((None, d, FC), lambda c: (layer, 0, c + start))
    tall = pl.BlockSpec((None, FC, d), lambda c: (layer, c + start, 0))
    blocks = [wide, wide, tall]
    gblock = pl.BlockSpec((8, None, 3, g.shape[3], FC), lambda c: (0, c, 0, 0, 0))
    size = 3 * d * FC * chunks
    return pl.pallas_call(
        functools.partial(adamw_body, sum(one.size for one in w)),
        grid=(chunks,),
        in_specs=[once((8, 128)), gblock, *blocks * 3] + [pl.BlockSpec(memory_space=pl.ANY)] * len(done),
        out_specs=blocks * 3,
        out_shape=[jax.ShapeDtypeStruct(o.shape, o.dtype) for o in (*w, *m, *v)],
        input_output_aliases={11 + i: i for i in range(len(done))},
        compiler_params=params(),
        cost_estimate=pl.CostEstimate(flops=120 * size, bytes_accessed=22 * size, transcendentals=size),
        name="adamw",
    )(squares, g, *w, *m, *v, *done)


def solution(mesh):
    def step(x, dy, *arrays):
        weights, m, v = (arrays[i : i + 3] for i in (0, 3, 6))
        x, dy = x[0], dy[0]
        gate, up, h = forward(0, x, *weights)
        shard1, so_far, by_h, early = last(1, h, dy, *weights)
        late = lax.all_gather(shard1[SPREAD:], "dp")
        shard0, squares = first(0, x, by_h, gate, up, weights[2], so_far)
        half = shard0.shape[0] // 2
        parts = [(1, 0, early), (1, SPREAD, late)]
        parts += [(0, start, lax.all_gather(part, "dp")) for start, part in ((0, shard0[:half]), (half, shard0[half:]))]
        new = ()
        for layer, start, part in parts:
            new = adamw(layer, start, squares, part, weights, m, v, new)
        return tuple(new)

    return jax.shard_map(
        step,
        mesh=mesh,
        in_specs=(P(("rep", "dp"), None, None),) * 2 + (P(None, None, None),) * 9,
        out_specs=(P("rep", None, None),) * 9,
        check_vma=False,
    )
```

time: 1300 us -> 754 us (0.58)
  Pallas kernels: 0 us -> 727 us
  waiting for transfers between devices: 576 us -> 0.11 us
  matrix products: 471 us -> 0 us
  other arithmetic: 215 us -> 0 us
    pallas_call x0 -> x7, Pallas kernels: none -> 727 us  [the longest x1 245 us: last(): pl.pallas_call(functools.partial(last_body, f, n), grid=(n + 3 * LAG,), i...]
    psum x1 -> x0, waiting for transfers between devices: 576 us -> none  [step(): summed[number] = [lax.psum(by_w[name], 'dp') for name in NAMES]]
    dot_general x15 -> x0, matrix products: 471 us -> none  [the longest x5 167 us: layer(): gate = jnp.dot(a, w['w_gate'], preferred_element_type=jnp.float32)]
    convert_element_type x2 -> x0, other arithmetic: 175 us -> none  [adamw(): return ((w - 0.02 * step).astype(jnp.bfloat16), m, v)]
    reduce_sum x4 -> x0, other arithmetic: 35.1 us -> none  [the longest x3 32.3 us: step(): jnp.sum(g * g)]
  transfers between devices with their start and end apart: 1 -> 3, of which waited for: 1 -> 0; matrix products, arithmetic and copies ran while one was open for 0% -> 1% of each run, Pallas kernels for 0% -> 47%
where the time goes in v1:
time: 754 us; the launch traced here: 750 us
  Pallas kernels  727 us (96%)
  between operations  14 us (2%)
  local copies, waits for them, and re-layouts  8.15 us (1%)
    pallas_call x1, Pallas kernels, last(): pl.pallas_call(functools.partial(last_body, f, n), grid=(n + 3 * LAG,), i...  245 us
    pallas_call x4, Pallas kernels, adamw(): pl.pallas_call(functools.partial(adamw_body, sum((one.size for one in w))...  225 us
    pallas_call x1, Pallas kernels, first(): pl.pallas_call(functools.partial(first_body, f, n), grid=(n + 3 * LAG,),...  182 us
    pallas_call x1, Pallas kernels, forward(): pl.pallas_call(functools.partial(fwd_body, f), grid=(n,), in_specs=[once(...  74.5 us
  transfers between devices with their start and end apart: 3, of which 0 were waited for; matrix products, arithmetic and copies ran while one was open for 1% of the time, Pallas kernels for 47%

profile of v1, /device:TPU:0, one launch (start us, length us, event | category | flops | bytes accessed | tf_op | source)
XLA Modules:
  0.0 749.5 jit_solution(2141584453063109861)
XLA Ops:
  7.2 0.0 all-gather.11.cloned.1.call-start
  7.2 74.5 %forward.1 = (f32[2048,4864]{1,0:T(8,128)}, f32[2048,4864]{1,0:T(8,128)}, bf16[2048,896]{1,0:T(8,128)(2,1)}) custom-call(bf16[2048,896]{1,0:T(8,128)(2,1)} %bitcast.9, bf16[2,896,4736]{2,1,0:T(8,128)(2,1)} %refs_0_.7, bf16[2,896,4736]{2,1,0:T(8,128)(2,1)} %refs_1_.7, bf16[2,4736,896]{2,1,0:T(8,128)(2,1)} %refs_2_.7), custom_call_target="tpu_custom_call" | custom-call | flops 52143587328 | bytes 96993280 | tf_op jit(solution)/shard_map/forward/pallas_call | solution.py:80
  81.7 245.2 %last.1 = (bf16[19,3,112,256]{3,2,1,0:T(8,128)(2,1)}, f32[112,256]{1,0:T(8,128)}, bf16[2048,896]{1,0:T(8,128)(2,1)}, bf16[8,10,3,112,256]{4,3,2,1,0:T(8,128)(2,1)}) custom-call(bf16[2048,896]{1,0:T(8,128)(2,1)} %get-tuple-element.45.h_ref, bf16[2048,896]{1,0:T(8,128)(2,1)} %bitcast.8, bf16[2,896,4736]{2,1,0:T(8,128)(2,1)} %refs_0_.7, ...), custom_call_target="tpu_custom_call" | custom-call | flops 139049566208 | bytes 42434560 | tf_op jit(solution)/shard_map/last/pallas_call | solution.py:322
  326.9 2.7 slice.11
  329.6 0.0 all-gather.11.cloned.1.call-update
  329.6 0.0 all-gather.9.cloned.1.call-start
  329.6 182.3 %first.1 = (bf16[19,3,112,256]{3,2,1,0:T(8,128)(2,1)}, f32[8,128]{1,0:T(8,128)}) custom-call(bf16[2048,896]{1,0:T(8,128)(2,1)} %bitcast.10, bf16[2048,896]{1,0:T(8,128)(2,1)} %get-tuple-element.46.dy_ref, f32[2048,4864]{1,0:T(8,128)} %get-tuple-element.47.g_ref, f32[2048,4864]{1,0:T(8,128)} %get-tuple-element.48.u_ref, bf16[2,4736,896]{2,1,0:T(8,128)(2,1)} %refs_2_.7, ...), custom_call_target="tpu_custom_call" | custom-call | flops 69524783104 | bytes 77594624 | tf_op jit(solution)/shard_map/first/pallas_call | solution.py:412
  511.9 2.7 slice.10
  514.6 0.0 all-gather.9.cloned.1.call-update
  514.7 0.0 all-gather.7.cloned.1.call-start
  514.7 2.8 slice.9
  517.5 0.0 all-gather.7.cloned.1.call-update
  517.5 59.2 %adamw.4 = (bf16[2,896,4736]{2,1,0:T(8,128)(2,1)}, bf16[2,896,4736]{2,1,0:T(8,128)(2,1)}, bf16[2,4736,896]{2,1,0:T(8,128)(2,1)}, f32[2,896,4736]{2,1,0:T(8,128)}...) custom-call(f32[8,128]{1,0:T(8,128)} %get-tuple-element.50.sum_ref, ...), custom_call_target="tpu_custom_call" | custom-call | flops 825753600 | bytes 151388160 | tf_op jit(solution)/shard_map/adamw/pallas_call | solution.py:464
  576.7 0.0 all-gather.11.cloned.1.call-done
  576.7 52.2 %adamw.5 = (bf16[2,896,4736]{2,1,0:T(8,128)(2,1)}, bf16[2,896,4736]{2,1,0:T(8,128)(2,1)}, bf16[2,4736,896]{2,1,0:T(8,128)(2,1)}, f32[2,896,4736]{2,1,0:T(8,128)}...) custom-call(f32[8,128]{1,0:T(8,128)} %get-tuple-element.50.sum_ref, ...), custom_call_target="tpu_custom_call", output_to_operand_aliasing={{0}: (11, {}), {1}: (12, {}), {2}: (13, {}), {3}: (14, {}),... | custom-call | flops 743178240 | bytes 136249344 | tf_op jit(solution)/shard_map/adamw/pallas_call | solution.py:464
  628.9 0.0 all-gather.9.cloned.1.call-done
  629.0 55.6 %adamw.6 = (bf16[2,896,4736]{2,1,0:T(8,128)(2,1)}, bf16[2,896,4736]{2,1,0:T(8,128)(2,1)}, bf16[2,4736,896]{2,1,0:T(8,128)(2,1)}, f32[2,896,4736]{2,1,0:T(8,128)}...) custom-call(f32[8,128]{1,0:T(8,128)} %get-tuple-element.50.sum_ref, ...), custom_call_target="tpu_custom_call", output_to_operand_aliasing={{0}: (11, {}), {1}: (12, {}), {2}: (13, {}), {3}: (14, {}),... | custom-call | flops 743178240 | bytes 136249344 | tf_op jit(solution)/shard_map/adamw/pallas_call | solution.py:464
  684.6 0.0 all-gather.7.cloned.1.call-done
  684.6 58.1 %adamw.7 = (bf16[2,896,4736]{2,1,0:T(8,128)(2,1)}, bf16[2,896,4736]{2,1,0:T(8,128)(2,1)}, bf16[2,4736,896]{2,1,0:T(8,128)(2,1)}, f32[2,896,4736]{2,1,0:T(8,128)}...) custom-call(f32[8,128]{1,0:T(8,128)} %get-tuple-element.50.sum_ref, ...), custom_call_target="tpu_custom_call", output_to_operand_aliasing={{0}: (11, {}), {1}: (12, {}), {2}: (13, {}), {3}: (14, {}),... | custom-call | flops 825753600 | bytes 151388160 | tf_op jit(solution)/shard_map/adamw/pallas_call | solution.py:464
Async XLA Ops:
  7.2 569.6 %all-gather.11.cloned.1.call-start = ((), (), s32[]{:S(2)}) async-start(), calls=%async_computation.2 | async-start | bytes 13934592 | tf_op jit(solution)/shard_map/all_gather | solution.py:483
  329.6 299.4 %all-gather.9.cloned.1.call-start = ((), (), s32[]{:S(2)}) async-start(), calls=%async_computation.1 | async-start | bytes 13934592 | tf_op jit(solution)/shard_map/all_gather | solution.py:487
  514.7 170.0 %all-gather.7.cloned.1.call-start = ((), (), s32[]{:S(2)}) async-start(), calls=%async_computation | async-start | bytes 15482880 | tf_op jit(solution)/shard_map/all_gather | solution.py:487
Sparse Core Ops, SparseCore 0:
  329.7 97.6 all-gather.10
  514.8 65.6 all-gather.8
  582.3 71.2 all-gather.6

commit v2 on v1

--- a/solution.py
+++ b/solution.py
@@ -10,8 +10,8 @@
 BF, F32 = jnp.bfloat16, jnp.float32
 FC = 256
 TM = 512
-LIMIT = 62 * 1024 * 1024
-SPREAD = 10
+LIMIT = 67_043_328
+STARTS = (16, 28)
 LAG = 2
 SLOTS = 4
 
@@ -91,14 +91,13 @@
 
 
 class Sum:
-    def __init__(self, n, rows, out_ref, ss_ref, refs, spread=0, whole_ref=None):
-        self.n, self.rows, self.out, self.ss = n, rows, out_ref, ss_ref
+    def __init__(self, n, rows, out_refs, ss_ref, refs, spread, whole_ref):
+        self.n, self.rows, self.outs, self.ss = n, rows, out_refs, ss_ref
         self.spread, self.whole = spread, whole_ref
         self.own, self.land0, self.send1, self.keep1, self.land1, self.send2, self.keep2, self.land2 = refs[:8]
         self.sends, self.lands = refs[8:14:2], refs[9:14:2]
-        if spread:
-            self.fin, self.local, *sems = refs[14:]
-            self.out_sends, self.out_lands = sems[::2], sems[1::2]
+        self.fin, self.local, *sems = refs[14:]
+        self.out_sends, self.out_lands = sems[::2], sems[1::2]
         me = self.me = lax.axis_index("dp")
         self.x, self.y, self.core = me // 4, (me // 2) % 2, me % 2
         self.over = (me + 1 - 2 * self.core, me + 4 - 8 * self.x, me + 2 - 4 * self.y)
@@ -178,7 +177,7 @@
         ]
 
     def receive(self, c):
-        for stage in (2, 1, 0) if self.spread else ():
+        for stage in (2, 1, 0):
             k = c - (4 + stage) * LAG
 
             @self.when(k, self.spread)
@@ -194,9 +193,13 @@
         def _():
             self.copy(2, k2).wait()
             g = (self.keep2[lax.rem(k2, 2)] + self.land2[lax.rem(k2, SLOTS)].astype(F32)).astype(BF)
-            self.out[...] = g
-            if self.spread:
-                self.fin[lax.rem(k2, 2)] = g
+            self.fin[lax.rem(k2, 2)] = g
+            for start, end, out_ref in self.outs:
+
+                @pl.when((k2 >= start) & (k2 < end))
+                def _(out_ref=out_ref):
+                    out_ref[...] = g
+
             g = g.astype(F32)
             self.ss[...] += g[0] * g[0] + g[1] * g[1] + g[2] * g[2]
 
@@ -221,15 +224,20 @@
             for to, place in ((0, 2 - odd), (1, 3)):
                 self.send1[two, :, to] = (self.own[two, 0, :, place].astype(F32) + self.land0[four, :, place].astype(F32)).astype(BF)
 
+    def send_own(self, c):
+        @self.when(c)
+        def _():
+            self.copy(0, c).start()
+
     def send(self, c):
-        for stage in range(3):
+        for stage in (1, 2):
             k = c - stage * LAG
 
             @self.when(k)
             def _(stage=stage, k=k):
                 self.copy(stage, k).start()
 
-        for stage in range(3 if self.spread else 0):
+        for stage in range(3):
             k = c - (3 + stage) * LAG
 
             @self.when(k, self.spread)
@@ -265,20 +273,31 @@
     return (by_a * scale - h * (scale**3 * jnp.mean(by_a * h, -1, keepdims=True))).astype(BF)
 
 
-def last_body(width, n, h_ref, dy_ref, wg_ref, wu_ref, wd_ref, out_ref, ss_ref, by_ref, whole_ref, a_ref, at_ref, dyt_ref, da_ref, ws, wds, dgu, hid, *refs):
+def middle_body(
+    width, n, starts, h_ref, x_ref, dy_ref, wg_ref, wu_ref, wd_ref, g_ref, u_ref, whole_ref, out1_ref, out2_ref, sum_ref,
+    ss, hx, a, at, dyt, da, ws, wds, dgu, hid, part, landed, part_sent, part_landed, load, *refs,
+):
     c = pl.program_id(0)
-    total = Sum(n, out_ref.shape[1], out_ref, ss_ref, refs, SPREAD, whole_ref)
+    total = Sum(2 * n, out1_ref.shape[1], tuple(zip(starts, (starts[1], 2 * n), (out1_ref, out2_ref), strict=True)), ss, refs, starts[0], whole_ref)
+    tiles = dy_ref.shape[0] // TM
+
+    def fetch(ref):
+        copy = pltpu.make_async_copy(ref, hx, load)
+        copy.start()
+        copy.wait()
 
     @pl.when(c == 0)
     def _():
         total.enter()
-        da_ref[...] = jnp.zeros_like(da_ref)
-        ss_ref[...] = jnp.zeros_like(ss_ref)
-        a_ref[...] = normed(h_ref[...])
-        turn(at_ref, lambda rows: a_ref[rows, :])
-        turn(dyt_ref, lambda rows: dy_ref[rows, :])
+        fetch(h_ref)
+        da[...] = jnp.zeros_like(da)
+        ss[...] = jnp.zeros_like(ss)
+        a[...] = normed(hx[...])
+        turn(at, lambda rows: a[rows, :])
+        turn(dyt, lambda rows: dy_ref[rows, :])
 
     total.receive(c)
+    total.send(c)
 
     @pl.when(c < n)
     def _():
@@ -286,107 +305,60 @@
         ws[:, FC:] = masked(c, width, 1, wu_ref[...])
         wds[...] = masked(c, width, 0, wd_ref[...])
 
-        def tile(i, _):
-            rows = pl.ds(pl.multiple_of(i * TM, TM), TM)
-            gu = nn(a_ref[rows, :], ws[...])
-            dh = nt(dy_ref[rows, :], wds[...]).astype(BF).astype(F32)
-            h, dg, du = back(gu[:, :FC], gu[:, FC:], dh)
+        def heads(rows):
+            return nn(a[rows, :], ws[...]), nt(dy_ref[rows, :], wds[...])
+
+        def tail(rows):
+            da[rows, :] += nt(dgu[rows, :], ws[...])
+
+        places = [slice(i * TM, (i + 1) * TM) for i in range(tiles)]
+        ahead = heads(places[0])
+        for i, rows in enumerate(places):
+            gu, dh = ahead
+            if i + 1 < tiles:
+                ahead = heads(places[i + 1])
+            h, dg, du = back(gu[:, :FC], gu[:, FC:], dh.astype(BF).astype(F32))
             hid[rows, :] = h
             dgu[rows, :FC] = dg
             dgu[rows, FC:] = du
-            da_ref[rows, :] += nt(dgu[rows, :], ws[...])
-            return 0
-
-        lax.fori_loop(0, a_ref.shape[0] // TM, tile, 0, unroll=True)
-        gradients(total, c, at_ref, dyt_ref, dgu, hid)
-
-    total.send(c)
+            if i:
+                tail(places[i - 1])
+        tail(places[-1])
+        gradients(total, c, at, dyt, dgu, hid)
 
     @pl.when(c == n)
     def _():
         def tile(i, _):
             rows = pl.ds(pl.multiple_of(i * TM, TM), TM)
-            by_ref[rows, :] = dy_ref[rows, :] + by_normed(h_ref[rows, :], da_ref[rows, :])
+            a[rows, :] = dy_ref[rows, :] + by_normed(hx[rows, :], da[rows, :])
             return 0
 
-        lax.fori_loop(0, by_ref.shape[0] // TM, tile, 0)
-
-
-def last(layer, h, dy, w_gate, w_up, w_down):
-    t, d = h.shape
-    f = w_gate.shape[2]
-    n = pl.cdiv(f, FC)
-    rows = d // 8
-    wcol = pl.BlockSpec((None, d, FC), lambda c: (layer, 0, jnp.minimum(c, n - 1)))
-    wrow = pl.BlockSpec((None, FC, d), lambda c: (layer, jnp.minimum(c, n - 1), 0))
-    return pl.pallas_call(
-        functools.partial(last_body, f, n),
-        grid=(n + 3 * LAG,),
-        in_specs=[once((t, d)), once((t, d)), wcol, wcol, wrow],
-        out_specs=[
-            pl.BlockSpec((None, 3, rows, FC), lambda c: (jnp.maximum(c - 3 * LAG, 0), 0, 0, 0)),
-            pl.BlockSpec((rows, FC), lambda c: (0, 0)),
-            once((t, d)),
-            pl.BlockSpec(memory_space=pl.ANY),
-        ],
-        out_shape=[
-            jax.ShapeDtypeStruct((n, 3, rows, FC), BF),
-            jax.ShapeDtypeStruct((rows, FC), F32),
-            jax.ShapeDtypeStruct((t, d), BF),
-            jax.ShapeDtypeStruct((8, SPREAD, 3, rows, FC), BF),
-        ],
-        scratch_shapes=[
-            pltpu.VMEM((t, d), BF),
-            pltpu.VMEM((d, t), BF),
-            pltpu.VMEM((d, t), BF),
-            pltpu.VMEM((t, d), F32),
-            pltpu.VMEM((d, 2 * FC), BF),
-            pltpu.VMEM((FC, d), BF),
-            pltpu.VMEM((t, 2 * FC), BF),
-            pltpu.VMEM((t, FC), BF),
-            *Sum.scratch(rows),
-            *Sum.spread_scratch(rows),
-        ],
-        compiler_params=params(collective_id=0, has_side_effects=True),
-        cost_estimate=pl.CostEstimate(flops=16 * t * d * f, bytes_accessed=10 * d * f, transcendentals=t * f),
-        name="last",
-    )(h, dy, w_gate, w_up, w_down)
-
-
-def first_body(width, n, x_ref, dy_ref, g_ref, u_ref, wd_ref, so_far_ref, out_ref, sum_ref, ss_ref, at_ref, dyt_ref, wds, dgu, hid, part, landed, part_sent, part_landed, *refs):
-    c = pl.program_id(0)
-    total = Sum(n, out_ref.shape[1], out_ref, ss_ref, refs)
-
-    @pl.when(c == 0)
-    def _():
-        total.enter()
-        ss_ref[...] = so_far_ref[...]
-        turn(at_ref, lambda rows: normed(x_ref[rows, :]))
-        turn(dyt_ref, lambda rows: dy_ref[rows, :])
-
-    total.receive(c)
-
-    @pl.when(c < n)
-    def _():
-        wds[...] = masked(c, width, 0, wd_ref[...])
+        lax.fori_loop(0, tiles, tile, 0)
+        fetch(x_ref)
+        turn(at, lambda rows: normed(hx[rows, :]))
+        turn(dyt, lambda rows: a[rows, :])
+
+    @pl.when((c >= n) & (c < 2 * n))
+    def _():
+        wds[...] = masked(c - n, width, 0, wd_ref[...])
 
         def tile(i, _):
             rows = pl.ds(pl.multiple_of(i * TM, TM), TM)
-            dh = nt(dy_ref[rows, :], wds[...]).astype(BF).astype(F32)
+            dh = nt(a[rows, :], wds[...]).astype(BF).astype(F32)
             h, dg, du = back(g_ref[rows, :], u_ref[rows, :], dh)
             hid[rows, :] = h
             dgu[rows, :FC] = dg
             dgu[rows, FC:] = du
             return 0
 
-        lax.fori_loop(0, dy_ref.shape[0] // TM, tile, 0, unroll=True)
-        gradients(total, c, at_ref, dyt_ref, dgu, hid)
-
-    total.send(c)
-
-    @pl.when(c == n + 3 * LAG - 1)
-    def _():
-        part[0] = jnp.full(part.shape[1:], jnp.sum(ss_ref[...]))
+        lax.fori_loop(0, tiles, tile, 0, unroll=True)
+        gradients(total, c, at, dyt, dgu, hid)
+
+    total.send_own(c)
+
+    @pl.when(c == 2 * n + 3 * LAG - 1)
+    def _():
+        part[0] = jnp.full(part.shape[1:], jnp.sum(ss[...]))
         for stage in range(3):
             copy = pltpu.make_async_remote_copy(
                 src_ref=part.at[stage],
@@ -402,26 +374,37 @@
         sum_ref[...] = part[3]
 
 
-def first(layer, x, dy, g, u, w_down, so_far):
-    t, d = dy.shape
-    f = w_down.shape[1]
+def middle(h, x, dy, g, u, w_gate, w_up, w_down, starts):
+    t, d = h.shape
+    f = w_gate.shape[2]
     n = pl.cdiv(f, FC)
     rows = d // 8
-    gu = pl.BlockSpec((t, FC), lambda c: (0, jnp.minimum(c, n - 1)))
-    wrow = pl.BlockSpec((None, FC, d), lambda c: (layer, jnp.minimum(c, n - 1), 0))
+    wcol = pl.BlockSpec((None, d, FC), lambda c: (1, 0, jnp.minimum(c, n - 1)))
+    wrow = pl.BlockSpec((None, FC, d), lambda c: (1 - jnp.minimum(c // n, 1), jnp.minimum(c - n * jnp.minimum(c // n, 1), n - 1), 0))
+    gu = pl.BlockSpec((t, FC), lambda c: (0, jnp.clip(c - n, 0, n - 1)))
+    sizes = starts[1] - starts[0], 2 * n - starts[1]
+    outs = [
+        pl.BlockSpec((None, 3, rows, FC), lambda c, i=i: (jnp.clip(c - 3 * LAG - starts[i], 0, sizes[i] - 1), 0, 0, 0)) for i in range(2)
+    ]
+    anywhere = pl.BlockSpec(memory_space=pl.ANY)
     return pl.pallas_call(
-        functools.partial(first_body, f, n),
-        grid=(n + 3 * LAG,),
-        in_specs=[once((t, d)), once((t, d)), gu, gu, wrow, once((rows, FC))],
-        out_specs=[
-            pl.BlockSpec((None, 3, rows, FC), lambda c: (jnp.maximum(c - 3 * LAG, 0), 0, 0, 0)),
-            once((8, 128)),
+        functools.partial(middle_body, f, n, starts),
+        grid=(2 * n + 3 * LAG,),
+        in_specs=[anywhere, anywhere, once((t, d)), wcol, wcol, wrow, gu, gu],
+        out_specs=[anywhere, *outs, once((8, 128))],
+        out_shape=[
+            jax.ShapeDtypeStruct((8, starts[0], 3, rows, FC), BF),
+            *(jax.ShapeDtypeStruct((size, 3, rows, FC), BF) for size in sizes),
+            jax.ShapeDtypeStruct((8, 128), F32),
         ],
-        out_shape=[jax.ShapeDtypeStruct((n, 3, rows, FC), BF), jax.ShapeDtypeStruct((8, 128), F32)],
         scratch_shapes=[
             pltpu.VMEM((rows, FC), F32),
+            pltpu.VMEM((t, d), BF),
+            pltpu.VMEM((t, d), BF),
             pltpu.VMEM((d, t), BF),
             pltpu.VMEM((d, t), BF),
+            pltpu.VMEM((t, d), F32),
+            pltpu.VMEM((d, 2 * FC), BF),
             pltpu.VMEM((FC, d), BF),
             pltpu.VMEM((t, 2 * FC), BF),
             pltpu.VMEM((t, FC), BF),
@@ -429,35 +412,48 @@
             pltpu.VMEM((3, 8, 128), F32),
             pltpu.SemaphoreType.DMA((3,)),
             pltpu.SemaphoreType.DMA((3,)),
+            pltpu.SemaphoreType.DMA,
             *Sum.scratch(rows),
+            *Sum.spread_scratch(rows),
         ],
-        compiler_params=params(collective_id=1, has_side_effects=True),
-        cost_estimate=pl.CostEstimate(flops=8 * t * d * f, bytes_accessed=8 * t * f, transcendentals=t * f),
-        name="first",
-    )(x, dy, g, u, w_down, so_far)
+        compiler_params=params(collective_id=0, has_side_effects=True),
+        cost_estimate=pl.CostEstimate(flops=24 * t * d * f, bytes_accessed=8 * t * f, transcendentals=2 * t * f),
+        name="middle",
+    )(h, x, dy, w_gate, w_up, w_down, g, u)
 
 
 def adamw_body(count, sum_ref, g_ref, *refs):
     ins, outs = refs[:9], refs[-9:]
     factor = jnp.minimum(1.0, 0.5 * lax.rsqrt(sum_ref[0:1, 0:1] / count + 1e-30))
-    for i in range(3):
+
+    def update(i, g, place):
         w_ref, m_ref, v_ref = ins[i::3]
         w_out, m_out, v_out = outs[i::3]
-        g = g_ref[:, i].reshape(-1, FC)
-        g = (g.T if i == 2 else g).astype(F32) * factor
-        m = 0.9 * m_ref[...] + 0.1 * g
-        v = 0.95 * v_ref[...] + 0.05 * g * g
-        w = w_ref[...].astype(F32)
-        m_out[...] = m
-        v_out[...] = v
-        w_out[...] = (w - 0.02 * (m * lax.rsqrt(v + 1e-8) + 0.1 * w)).astype(BF)
-
-
-def adamw(layer, start, squares, g, w, m, v, done):
+        g = g.astype(F32) * factor
+        m = 0.9 * m_ref[place] + 0.1 * g
+        v = 0.95 * v_ref[place] + 0.05 * g * g
+        w = w_ref[place].astype(F32)
+        m_out[place] = m
+        v_out[place] = v
+        w_out[place] = (w - 0.02 * (m * lax.rsqrt(v + 1e-8) + 0.1 * w)).astype(BF)
+
+    rows = g_ref.shape[2]
+
+    def block(j, _):
+        for i in range(2):
+            update(i, g_ref[j, i], (pl.ds(pl.multiple_of(j * rows, rows), rows), slice(None)))
+        return 0
+
+    lax.fori_loop(0, 8, block, 0)
+    for j in range(0, FC, 128):
+        update(2, g_ref[:, 2, :, j : j + 128].reshape(-1, 128).T, (slice(j, j + 128), slice(None)))
+
+
+def adamw(start, squares, g, w, m, v, done):
     d, f = w[0].shape[1:]
-    chunks = g.shape[1]
-    wide = pl.BlockSpec((None, d, FC), lambda c: (layer, 0, c + start))
-    tall = pl.BlockSpec((None, FC, d), lambda c: (layer, c + start, 0))
+    n, chunks = pl.cdiv(f, FC), g.shape[1]
+    wide = pl.BlockSpec((None, d, FC), lambda c: (1 - (c + start) // n, 0, lax.rem(c + start, n)))
+    tall = pl.BlockSpec((None, FC, d), lambda c: (1 - (c + start) // n, lax.rem(c + start, n), 0))
     blocks = [wide, wide, tall]
     gblock = pl.BlockSpec((8, None, 3, g.shape[3], FC), lambda c: (0, c, 0, 0, 0))
     size = 3 * d * FC * chunks
@@ -479,15 +475,11 @@
         weights, m, v = (arrays[i : i + 3] for i in (0, 3, 6))
         x, dy = x[0], dy[0]
         gate, up, h = forward(0, x, *weights)
-        shard1, so_far, by_h, early = last(1, h, dy, *weights)
-        late = lax.all_gather(shard1[SPREAD:], "dp")
-        shard0, squares = first(0, x, by_h, gate, up, weights[2], so_far)
-        half = shard0.shape[0] // 2
-        parts = [(1, 0, early), (1, SPREAD, late)]
-        parts += [(0, start, lax.all_gather(part, "dp")) for start, part in ((0, shard0[:half]), (half, shard0[half:]))]
+        whole, one, two, squares = middle(h, x, dy, gate, up, *weights, STARTS)
+        parts = [(0, whole), (STARTS[0], lax.all_gather(one, "dp")), (STARTS[1], lax.all_gather(two, "dp"))]
         new = ()
-        for layer, start, part in parts:
-            new = adamw(layer, start, squares, part, weights, m, v, new)
+        for start, part in parts:
+            new = adamw(start, squares, part, weights, m, v, new)
         return tuple(new)
 
     return jax.shard_map(

time: 754 us -> 661 us (0.88)
  Pallas kernels: 727 us -> 636 us
  waiting for transfers between devices: 0.11 us -> 11.2 us
  local copies, waits for them, and re-layouts: 8.15 us -> 0 us
    pallas_call x2 -> x1, Pallas kernels: 427 us -> 365 us  [middle(): pl.pallas_call(functools.partial(middle_body, f, n, starts), grid=(2 * n...]
    pallas_call x4 -> x3, Pallas kernels: 225 us -> 196 us  [adamw(): pl.pallas_call(functools.partial(adamw_body, sum((one.size for one in w))...]
    all_gather x3 -> x2, waiting for transfers between devices: 0.06 us -> 10.5 us  [the longest x1 10.5 us: step(): lax.all_gather(two, 'dp')]
    slice x3 -> x0, local copies, waits for them, and re-layouts: 8.15 us -> none  [the longest x1 2.79 us: step(): shard0[half:]]
  transfers between devices with their start and end apart: 3 -> 2, of which waited for: 0 -> 1; matrix products, arithmetic and copies ran while one was open for 1% -> 0% of each run, Pallas kernels for 47% -> 22%
where the time goes in v2:
time: 661 us
  Pallas kernels  636 us (96%)
  between operations  14.1 us (2%)
  waiting for transfers between devices  11.2 us (2%)
    pallas_call x1, Pallas kernels, middle(): pl.pallas_call(functools.partial(middle_body, f, n, starts), grid=(2 * n...  365 us
    pallas_call x3, Pallas kernels, adamw(): pl.pallas_call(functools.partial(adamw_body, sum((one.size for one in w))...  196 us
    pallas_call x1, Pallas kernels, forward(): pl.pallas_call(functools.partial(fwd_body, f), grid=(n,), in_specs=[once(...  74.5 us
  transfers between devices with their start and end apart: 2, of which 1 were waited for; matrix products, arithmetic and copies ran while one was open for 0% of the time, Pallas kernels for 22%

profile of v2, /device:TPU:0, one launch (start us, length us, event | category | flops | bytes accessed | tf_op | source)
XLA Modules:
  0.0 660.9 jit_solution(1711923401161574822)
XLA Ops:
  7.2 0.0 all-gather.7.cloned.1.call-start
  7.2 74.5 %forward.1 = (f32[2048,4864]{1,0:T(8,128)}, f32[2048,4864]{1,0:T(8,128)}, bf16[2048,896]{1,0:T(8,128)(2,1)}) custom-call(bf16[2048,896]{1,0:T(8,128)(2,1)} %bitcast.6, bf16[2,896,4736]{2,1,0:T(8,128)(2,1)} %refs_0_.5, bf16[2,896,4736]{2,1,0:T(8,128)(2,1)} %refs_1_.5, bf16[2,4736,896]{2,1,0:T(8,128)(2,1)} %refs_2_.5), custom_call_target="tpu_custom_call" | custom-call | flops 52143587328 | bytes 96993280 | tf_op jit(solution)/shard_map/forward/pallas_call | solution.py:80
  81.7 365.4 %middle.1 = (bf16[8,16,3,112,256]{4,3,2,1,0:T(8,128)(2,1)}, bf16[12,3,112,256]{3,2,1,0:T(8,128)(2,1)}, bf16[10,3,112,256]{3,2,1,0:T(8,128)(2,1)}, f32[8,128]{1,0:T(8,128)}) custom-call(bf16[2048,896]{1,0:T(8,128)(2,1)} %get-tuple-element.34.h_ref, bf16[2048,896]{1,0:T(8,128)(2,1)} %bitcast.7, bf16[2048,896]{1,0:T(8,128)(2,1)} %bitcast.8, ...), custom_call_target="tpu_custom_call" | custom-call | flops 208574349312 | bytes 77594624 | tf_op jit(solution)/shard_map/middle/pallas_call | solution.py:390
  447.1 0.0 all-gather.7.cloned.1.call-update
  447.1 0.0 all-gather.5.cloned.1.call-start
  447.2 0.7 all-gather.5.cloned.1.call-update
  447.9 82.7 %adamw.3 = (bf16[2,896,4736]{2,1,0:T(8,128)(2,1)}, bf16[2,896,4736]{2,1,0:T(8,128)(2,1)}, bf16[2,4736,896]{2,1,0:T(8,128)(2,1)}, f32[2,896,4736]{2,1,0:T(8,128)}...) custom-call(f32[8,128]{1,0:T(8,128)} %get-tuple-element.37.sum_ref, ...), custom_call_target="tpu_custom_call" | custom-call | flops 1321205760 | bytes 242221056 | tf_op jit(solution)/shard_map/adamw/pallas_call | solution.py:460
  530.6 0.0 all-gather.7.cloned.1.call-done
  530.6 62.3 %adamw.4 = (bf16[2,896,4736]{2,1,0:T(8,128)(2,1)}, bf16[2,896,4736]{2,1,0:T(8,128)(2,1)}, bf16[2,4736,896]{2,1,0:T(8,128)(2,1)}, f32[2,896,4736]{2,1,0:T(8,128)}...) custom-call(f32[8,128]{1,0:T(8,128)} %get-tuple-element.37.sum_ref, ...), custom_call_target="tpu_custom_call", output_to_operand_aliasing={{0}: (11, {}), {1}: (12, {}), {2}: (13, {}), {3}: (14, {}),... | custom-call | flops 990904320 | bytes 181665792 | tf_op jit(solution)/shard_map/adamw/pallas_call | solution.py:460
  593.0 10.5 %all-gather.5.cloned.1.call-done = bf16[80,3,112,256]{3,2,1,0:T(8,128)(2,1)} async-done(((bf16[10,3,112,256]{3,2,1,0:T(8,128)(2,1)}), bf16[80,3,112,256]{3,2,1,0:T(8,128)(2,1)}) %all-gather.5.cloned.1.call-update) | async-done | bytes 13762576 | tf_op jit(solution)/shard_map/all_gather | solution.py:479
  603.4 50.7 %adamw.5 = (bf16[2,896,4736]{2,1,0:T(8,128)(2,1)}, bf16[2,896,4736]{2,1,0:T(8,128)(2,1)}, bf16[2,4736,896]{2,1,0:T(8,128)(2,1)}, f32[2,896,4736]{2,1,0:T(8,128)}...) custom-call(f32[8,128]{1,0:T(8,128)} %get-tuple-element.37.sum_ref, ...), custom_call_target="tpu_custom_call", output_to_operand_aliasing={{0}: (11, {}), {1}: (12, {}), {2}: (13, {}), {3}: (14, {}),... | custom-call | flops 825753600 | bytes 151388160 | tf_op jit(solution)/shard_map/adamw/pallas_call | solution.py:460
Async XLA Ops:
  7.2 523.4 %all-gather.7.cloned.1.call-start = ((), (), s32[]{:S(2)}) async-start(), calls=%async_computation.1 | async-start | bytes 18579456 | tf_op jit(solution)/shard_map/all_gather | solution.py:479
  447.1 156.3 %all-gather.5.cloned.1.call-start = ((), (), s32[]{:S(2)}) async-start(), calls=%async_computation | async-start | bytes 15482880 | tf_op jit(solution)/shard_map/all_gather | solution.py:479
Sparse Core Ops, SparseCore 0:
  447.2 82.9 all-gather.6
  532.1 71.2 all-gather.4

commit v3 on v2

--- a/solution.py
+++ b/solution.py
@@ -11,7 +11,7 @@
 FC = 256
 TM = 512
 LIMIT = 67_043_328
-STARTS = (16, 28)
+STARTS = (16, 29)
 LAG = 2
 SLOTS = 4
 

time: 661 us -> 657 us (level)
    all_gather x1, waiting for transfers between devices: 10.5 us -> 2.65 us  [step(): lax.all_gather(two, 'dp')]
  transfers between devices with their start and end apart: 2 -> 2, of which waited for: 1 -> 2; matrix products, arithmetic and copies ran while one was open for 0% -> 0% of each run, Pallas kernels for 22% -> 22%
where the time goes in v3:
time: 657 us
  Pallas kernels  634 us (96%)
  between operations  14.1 us (2%)
  waiting for transfers between devices  8.89 us (1%)
    pallas_call x1, Pallas kernels, middle(): pl.pallas_call(functools.partial(middle_body, f, n, starts), grid=(2 * n...  365 us
    pallas_call x3, Pallas kernels, adamw(): pl.pallas_call(functools.partial(adamw_body, sum((one.size for one in w))...  194 us
    pallas_call x1, Pallas kernels, forward(): pl.pallas_call(functools.partial(fwd_body, f), grid=(n,), in_specs=[once(...  74.5 us
  transfers between devices with their start and end apart: 2, of which 2 were waited for; matrix products, arithmetic and copies ran while one was open for 0% of the time, Pallas kernels for 22%

profile of v3, /device:TPU:0, one launch (start us, length us, event | category | flops | bytes accessed | tf_op | source)
XLA Modules:
  0.0 656.7 jit_solution(4245717510546368563)
XLA Ops:
  7.2 0.0 all-gather.7.cloned.1.call-start
  7.2 74.5 %forward.1 = (f32[2048,4864]{1,0:T(8,128)}, f32[2048,4864]{1,0:T(8,128)}, bf16[2048,896]{1,0:T(8,128)(2,1)}) custom-call(bf16[2048,896]{1,0:T(8,128)(2,1)} %bitcast.6, bf16[2,896,4736]{2,1,0:T(8,128)(2,1)} %refs_0_.5, bf16[2,896,4736]{2,1,0:T(8,128)(2,1)} %refs_1_.5, bf16[2,4736,896]{2,1,0:T(8,128)(2,1)} %refs_2_.5), custom_call_target="tpu_custom_call" | custom-call | flops 52143587328 | bytes 96993280 | tf_op jit(solution)/shard_map/forward/pallas_call | solution.py:80
  81.7 365.4 %middle.1 = (bf16[8,16,3,112,256]{4,3,2,1,0:T(8,128)(2,1)}, bf16[13,3,112,256]{3,2,1,0:T(8,128)(2,1)}, bf16[9,3,112,256]{3,2,1,0:T(8,128)(2,1)}, f32[8,128]{1,0:T(8,128)}) custom-call(bf16[2048,896]{1,0:T(8,128)(2,1)} %get-tuple-element.34.h_ref, bf16[2048,896]{1,0:T(8,128)(2,1)} %bitcast.7, bf16[2048,896]{1,0:T(8,128)(2,1)} %bitcast.8, ...), custom_call_target="tpu_custom_call" | custom-call | flops 208574349312 | bytes 77594624 | tf_op jit(solution)/shard_map/middle/pallas_call | solution.py:390
  447.1 0.0 all-gather.7.cloned.1.call-update
  447.1 0.0 all-gather.5.cloned.1.call-start
  447.2 0.7 all-gather.5.cloned.1.call-update
  447.9 82.7 %adamw.3 = (bf16[2,896,4736]{2,1,0:T(8,128)(2,1)}, bf16[2,896,4736]{2,1,0:T(8,128)(2,1)}, bf16[2,4736,896]{2,1,0:T(8,128)(2,1)}, f32[2,896,4736]{2,1,0:T(8,128)}...) custom-call(f32[8,128]{1,0:T(8,128)} %get-tuple-element.37.sum_ref, ...), custom_call_target="tpu_custom_call" | custom-call | flops 1321205760 | bytes 242221056 | tf_op jit(solution)/shard_map/adamw/pallas_call | solution.py:460
  530.6 5.5 all-gather.7.cloned.1.call-done
  536.1 64.7 %adamw.4 = (bf16[2,896,4736]{2,1,0:T(8,128)(2,1)}, bf16[2,896,4736]{2,1,0:T(8,128)(2,1)}, bf16[2,4736,896]{2,1,0:T(8,128)(2,1)}, f32[2,896,4736]{2,1,0:T(8,128)}...) custom-call(f32[8,128]{1,0:T(8,128)} %get-tuple-element.37.sum_ref, ...), custom_call_target="tpu_custom_call", output_to_operand_aliasing={{0}: (11, {}), {1}: (12, {}), {2}: (13, {}), {3}: (14, {}),... | custom-call | flops 1073479680 | bytes 196804608 | tf_op jit(solution)/shard_map/adamw/pallas_call | solution.py:460
  600.8 2.6 all-gather.5.cloned.1.call-done
  603.4 46.4 %adamw.5 = (bf16[2,896,4736]{2,1,0:T(8,128)(2,1)}, bf16[2,896,4736]{2,1,0:T(8,128)(2,1)}, bf16[2,4736,896]{2,1,0:T(8,128)(2,1)}, f32[2,896,4736]{2,1,0:T(8,128)}...) custom-call(f32[8,128]{1,0:T(8,128)} %get-tuple-element.37.sum_ref, ...), custom_call_target="tpu_custom_call", output_to_operand_aliasing={{0}: (11, {}), {1}: (12, {}), {2}: (13, {}), {3}: (14, {}),... | custom-call | flops 743178240 | bytes 136249344 | tf_op jit(solution)/shard_map/adamw/pallas_call | solution.py:460
Async XLA Ops:
  7.2 529.0 %all-gather.7.cloned.1.call-start = ((), (), s32[]{:S(2)}) async-start(), calls=%async_computation.1 | async-start | bytes 20127744 | tf_op jit(solution)/shard_map/all_gather | solution.py:479
  447.1 156.3 %all-gather.5.cloned.1.call-start = ((), (), s32[]{:S(2)}) async-start(), calls=%async_computation | async-start | bytes 13934592 | tf_op jit(solution)/shard_map/all_gather | solution.py:479
Sparse Core Ops, SparseCore 0:
  447.3 88.8 all-gather.6
  538.0 65.4 all-gather.4
